TPU v7x, 32 devices: a whole 2x2x4 slice. The times are simulated.
32 devices in a mesh: section: 4 (over y, core), wide: 2 (over x), narrow: 4 (over z).
Axes of the slice: x: 2, y: 2, z: 4, core: 2. Of those that a mesh axis runs over, the one named last changes fastest.
Arguments:
- normed_inputs: bfloat16 [4, 4, 4, 192, 4096], P('section', 'narrow', None, 'wide'), may hold values from -160 to 160
- value_cotangent: bfloat16 [4, 4, 4, 192, 1024], P('section', 'narrow', None, 'wide'), may hold values from -6 to 6
- expert_hidden: bfloat16 [4, 4, 4, 64, 7168], P('section', 'narrow', None, None, 'wide'), may hold values from -40 to 40
- expert_cotangent: bfloat16 [4, 4, 4, 64, 4096], P('section', 'narrow', None, 'wide'), may hold values from -110 to 110
- slot_gate: bfloat16 [4, 4, 4, 64], P('section', 'narrow', None, 'wide'), may hold values from 0.25 to 1
- slot_count: int32 [4, 4, 4], P('section', 'narrow'), may hold values from 33 to 64, as said below
- expert_weight: bfloat16 [4, 7168, 4096], P('section', 'wide', 'narrow'), may hold values from -0.0625 to 0.0625
- expert_moment: float32 [4, 7168, 4096], P('section', 'wide', 'narrow'), may hold values from -6 to 6
- value_weight: bfloat16 [4, 4096, 1024], P('section', ('wide', 'narrow')), may hold values from -0.09375 to 0.09375
- value_moment: float32 [4, 4096, 1024], P('section', ('wide', 'narrow')), may hold values from -6 to 6
Outputs:
- expert_weight_next: bfloat16 [4, 7168, 4096], P('section', 'wide', 'narrow')
- expert_moment_next: float32 [4, 7168, 4096], P('section', 'wide', 'narrow')
- value_weight_next: bfloat16 [4, 4096, 1024], P('section', ('wide', 'narrow'))
- value_moment_next: float32 [4, 4096, 1024], P('section', ('wide', 'narrow'))
Inputs may be any that keep to these rules, and one draw needn't show every extreme that they name: The live slots of a micro-batch are slots 0 to slot_count - 1; in every layer and replica some micro-batch fills all 64 slots.
All inputs are finite; a program needn't handle non-finite values.
Results may differ from a plain program's by a relative error of at most 0.014.
Values may be sent and summed in bfloat16 or wider, within the bound.
A program may use at most 192 MiB of HBM per device.

v0:
```python
import functools
import math

import jax
import jax.numpy as jnp
from jax import lax
from jax.experimental import pallas as pl
from jax.experimental.pallas import tpu as pltpu
from jax.sharding import PartitionSpec as P

MOMENTUM_DECAY = 0.9
STEP_RATE = 0.01
MESH = pl.DeviceIdType.MESH
F32 = jnp.float32
BF16 = jnp.bfloat16
RS_PIECES = 2


def column_chunks(width):
    lanes = width // 128
    return max(c for c in range(1, 9) if lanes % c == 0)


def grant(scratch, *arrays):
    held = [(math.prod(a.shape), a.dtype) for a in arrays]
    held += [(math.prod(a.inner_aval.shape), a.inner_aval.dtype) for a in scratch]
    return sum(n * d.itemsize for n, d in held) + 2 * 2**20


def dot_rows(a, b):
    return lax.dot_general(a, b, (((0,), (0,)), ((), ())), preferred_element_type=F32)


def gather_kernel(
    dims,
    x_ref,
    vc_ref,
    h_ref,
    cot_ref,
    coef_ref,
    mom_ref,
    *refs,
):
    n_section, n_wide, n_narrow, chunks = dims
    egrads, emoms, refs = refs[:chunks], refs[chunks : 2 * chunks], refs[2 * chunks :]
    run_gather(dims, x_ref, vc_ref, h_ref, cot_ref, coef_ref, mom_ref, egrads, emoms, *refs)


def run_gather(
    dims,
    x_ref,
    vc_ref,
    h_ref,
    cot_ref,
    coef_ref,
    mom_ref,
    egrads,
    emoms,
    vgrad,
    total,
    hbuf,
    sbuf,
    scaled,
    rows,
    cots,
    part,
    rbuf,
    rlast,
    sums,
    mine,
    h_recv,
    h_right,
    h_left,
    s_recv,
    s_send,
    s_relay,
    x_recv,
    x_send,
    r_recv,
    r_last,
    r_right,
    r_left,
    g_recv,
    g_send,
    local,
):
    n_section, n_wide, n_narrow, chunks = dims
    si, wi, ni = lax.axis_index("section"), lax.axis_index("wide"), lax.axis_index("narrow")
    last = n_narrow - 1
    tokens = x_ref.shape[0]
    h_rows = h_ref.shape[0]
    c_width = h_ref.shape[1] // chunks
    r_width = rows.shape[2]
    s_width = sbuf.shape[4]
    piece = r_width // RS_PIECES
    dest_order = [d for pair in zip(range(last, -1, -1), range(n_narrow)) for d in pair]
    dest_order = list(dict.fromkeys(dest_order))

    def at(section=0, wide=0, narrow=0):
        return (
            lax.rem(si + section, n_section),
            lax.rem(wi + wide, n_wide),
            lax.rem(ni + narrow, n_narrow),
        )

    def remote(src, dst, send_sem, recv_sem, device):
        return pltpu.make_async_remote_copy(
            src_ref=src,
            dst_ref=dst,
            send_sem=send_sem,
            recv_sem=recv_sem,
            device_id=device,
            device_id_type=MESH,
        )

    right, left = (si, wi, jnp.minimum(ni + 1, last)), (si, wi, jnp.maximum(ni - 1, 0))
    groups = [
        [(0, w, n) for w in range(n_wide) for n in range(n_narrow) if w or n],
        [(s, 0, 0) for s in range(1, n_section)],
    ]

    own = []
    own.append(
        pltpu.make_async_copy(vc_ref, cots.at[pl.ds(wi * tokens, tokens)], local.at[0])
    )
    for d in range(n_narrow):
        start = pl.multiple_of((wi * n_narrow + d) * r_width, r_width)
        own.append(
            pltpu.make_async_copy(
                x_ref.at[:, pl.ds(start, r_width)],
                rows.at[d, pl.ds(wi * tokens, tokens)],
                local.at[1 + d],
            )
        )
    own_hidden = [
        pltpu.make_async_copy(
            h_ref.at[:, pl.ds(c * c_width, c_width)],
            hbuf.at[c, pl.ds(ni * h_rows, h_rows)],
            local.at[1 + n_narrow + c],
        )
        for c in range(chunks)
    ]
    own_moment = [
        pltpu.make_async_copy(
            mom_ref.at[pl.ds(c * c_width, c_width)],
            emoms[c],
            local.at[1 + n_narrow + chunks + c],
        )
        for c in range(chunks)
    ]
    for copy in own + own_hidden:
        copy.start()

    barrier = pltpu.get_barrier_semaphore()
    n_peers = 0
    for group in groups:
        for offset in group:
            pl.semaphore_signal(barrier, inc=1, device_id=at(*offset), device_id_type=MESH)
            n_peers += 1
    pl.semaphore_wait(barrier, n_peers)

    def hidden_copy(r, c, rightward, first):
        block = hbuf.at[c, pl.ds(r * h_rows, h_rows)]
        src = h_ref.at[:, pl.ds(c * c_width, c_width)] if first else block
        sems = h_right if rightward else h_left
        return remote(src, block, sems.at[r, c], h_recv.at[r, c], right if rightward else left)

    def send_own_hidden(c):
        @pl.when(ni < last)
        def _():
            hidden_copy(ni, c, True, True).start()

        @pl.when(ni > 0)
        def _():
            hidden_copy(ni, c, False, True).start()

    def hidden_step(k, c):
        @pl.when(ni >= k)
        def _():
            hidden_copy(ni - k, c, True, False).wait_recv()

            @pl.when(ni < last)
            def _():
                hidden_copy(ni - k, c, True, False).start()

        @pl.when(ni + k <= last)
        def _():
            hidden_copy(ni + k, c, False, False).wait_recv()

            @pl.when(ni > 0)
            def _():
                hidden_copy(ni + k, c, False, False).start()

    def wide_vc(k, source):
        return remote(
            vc_ref,
            cots.at[pl.ds(source * tokens, tokens)],
            x_send.at[k, n_narrow],
            x_recv.at[source, n_narrow],
            at(0, k, 0),
        )

    def wide_rows(k, d, source):
        peer = lax.rem(wi + k, n_wide)
        start = pl.multiple_of((peer * n_narrow + d) * r_width, r_width)
        return remote(
            x_ref.at[:, pl.ds(start, r_width)],
            rows.at[d, pl.ds(source * tokens, tokens)],
            x_send.at[k, d],
            x_recv.at[source, d],
            at(0, k, 0),
        )

    def slot_copy(k):
        peer = lax.rem(ni + k, n_narrow)
        start = pl.multiple_of(peer * s_width, s_width)
        return remote(
            scaled.at[:, :, pl.ds(start, s_width)],
            sbuf.at[ni, :, wi],
            s_send.at[k],
            s_recv.at[ni, wi],
            at(0, 0, k),
        )

    def slot_relay(r, k):
        return remote(
            sbuf.at[r, :, wi],
            sbuf.at[r, :, wi],
            s_relay.at[r, k],
            s_recv.at[r, wi],
            at(0, k, 0),
        )

    def slot_arrival(r, w):
        return remote(sbuf.at[r, :, w], sbuf.at[r, :, w], s_send.at[0], s_recv.at[r, w], right)

    for k in range(1, n_wide):
        wide_vc(k, wi).start()
    for d in dest_order:
        for k in range(1, n_wide):
            wide_rows(k, d, wi).start()
    for c in range(0, 2):
        send_own_hidden(c)

    scaled[...] = (coef_ref[:, :, 0:1] * cot_ref[...].astype(F32)).astype(BF16)
    for k in range(1, n_narrow):
        slot_copy(k).start()
    for c in range(2, chunks):
        send_own_hidden(c)
    for copy in own_moment:
        copy.start()
    own_start = pl.multiple_of(ni * s_width, s_width)
    sbuf[ni, :, wi] = scaled[:, :, pl.ds(own_start, s_width)]
    for k in range(1, n_wide):
        slot_relay(ni, k).start()

    def make_part(d):
        if d == dest_order[0]:
            own[0].wait()
            for k in range(1, n_wide):
                wide_vc(k, lax.rem(wi + n_wide - k, n_wide)).wait_recv()
        own[1 + d].wait()
        for k in range(1, n_wide):
            wide_rows(k, d, lax.rem(wi + n_wide - k, n_wide)).wait_recv()
        part[d] = dot_rows(rows[d], cots[...]).astype(BF16)

    def piece_at(ref, d, q):
        return ref.at[d, pl.ds(q * piece, piece)]

    def sum_copy(d, q, rightward, final):
        dst = rlast.at[pl.ds(q * piece, piece)] if final else piece_at(rbuf, d, q)
        sem = r_last.at[q] if final else r_recv.at[d, q]
        sems = r_right if rightward else r_left
        return remote(piece_at(part, d, q), dst, sems.at[d, q], sem, right if rightward else left)

    def sum_send(i, d, rightward):
        final_right = rightward and d == i + 1
        for q in range(RS_PIECES):
            sum_copy(d, q, rightward, final_right).start()

    def sum_slot(slot):
        for i in range(1, n_narrow):
            j = slot - 2 * (i - 1)
            if j < 0 or j > last - i:
                continue
            for rightward in (True, False):
                me = i if rightward else last - i
                d = last - j if rightward else j

                @pl.when(ni == me)
                def _(me=me, d=d, rightward=rightward):
                    final = d == me
                    landing = final and rightward
                    for q in range(RS_PIECES):
                        sum_copy(d, q, rightward, landing).wait_recv()
                        rs = pl.ds(q * piece, piece)
                        came = rlast[rs] if landing else rbuf[d, rs]
                        if final:
                            vgrad[rs] += came.astype(F32)
                        else:
                            part[d, rs] = (part[d, rs].astype(F32) + came.astype(F32)).astype(BF16)
                            ahead = me + 1 if rightward else me - 1
                            sum_copy(d, q, rightward, rightward and d == ahead).start()

    def originate(d):
        if d > 0:

            @pl.when(ni == 0)
            def _():
                sum_send(0, d, True)

        if d < last:

            @pl.when(ni == last)
            def _():
                sum_send(last, d, False)

    mine[...] = jnp.zeros_like(mine)

    def add_squares(block):
        sq = block * block
        n_rows, n_cols = sq.shape
        folded = jnp.sum(sq.reshape(n_rows // 8, 8, n_cols), axis=0)
        acc = folded[:, 0:128]
        for lane in range(128, n_cols, 128):
            acc = acc + folded[:, lane : lane + 128]
        mine[...] += acc

    right_side = sbuf.at[...]

    def expert_chunk(c):
        product = dot_rows(hbuf[c], right_side[...].reshape(-1, s_width))
        egrads[c][...] = product
        add_squares(product)

    todo = list(dest_order)
    for k in range(1, n_narrow):
        for c in range(chunks):
            hidden_step(k, c)
            if k == 1 and c >= 3 and (c - 3) % 2 == 0 and len(todo) > 2:
                d = todo.pop(0)
                make_part(d)
                originate(d)
            if k == 2 and c == 1:
                while todo:
                    make_part(todo.pop(0))
                for d in dest_order[2:]:
                    if d > 0:

                        @pl.when(ni == 0)
                        def _(d=d):
                            sum_send(0, d, True)

                for d in dest_order[:1:-1]:
                    if d < last:

                        @pl.when(ni == last)
                        def _(d=d):
                            sum_send(last, d, False)

                vgrad[...] = part[ni].astype(F32)
            if k == 2 and c == 3:
                for j in range(1, n_narrow):
                    r = lax.rem(ni + n_narrow - j, n_narrow)
                    slot_arrival(r, wi).wait_recv()
                    for m in range(1, n_wide):
                        slot_relay(r, m).start()
            if k == 2 and c == chunks - 1:
                sum_slot(0)
                for copy in own_hidden:
                    copy.wait()
                for j in range(n_narrow):
                    for m in range(1, n_wide):
                        slot_arrival(j, lax.rem(wi + m, n_wide)).wait_recv()
            if k == 3:
                expert_chunk(c)
                if c % 2 == 1:
                    sum_slot(1 + c // 2)
    sum_slot(4)
    add_squares(vgrad[...])

    index = 0
    for group in groups:
        base = index
        for offset in group:
            remote(mine, sums.at[index], g_send.at[index], g_recv.at[index], at(*offset)).start()
            index += 1
        for i in range(base, index):
            remote(mine, sums.at[i], g_send.at[i], g_recv.at[i], right).wait_send()
        for i in range(base, index):
            remote(mine, sums.at[i], g_send.at[i], g_recv.at[i], right).wait_recv()
        mine[...] = mine[...] + jnp.sum(sums[base:index], axis=0)
    overall = jnp.sum(mine[...])
    total[...] = jnp.zeros_like(total) + overall

    for copy in own_moment:
        copy.wait()
    for c in range(chunks):
        for k in range(n_narrow):

            @pl.when((ni >= k) & (ni < last))
            def _(k=k, c=c):
                hidden_copy(ni - k, c, True, False).wait_send()

            @pl.when((ni + k <= last) & (ni > 0))
            def _(k=k, c=c):
                hidden_copy(ni + k, c, False, False).wait_send()

    for k in range(1, n_wide):
        wide_vc(k, wi).wait_send()
        for d in range(n_narrow):
            wide_rows(k, d, wi).wait_send()
        for r in range(n_narrow):
            slot_relay(r, k).wait_send()
    for k in range(1, n_narrow):
        slot_copy(k).wait_send()
    for d in range(n_narrow):
        for q in range(RS_PIECES):

            @pl.when(ni < d)
            def _(d=d, q=q):
                sum_copy(d, q, True, False).wait_send()

            @pl.when(ni > d)
            def _(d=d, q=q):
                sum_copy(d, q, False, False).wait_send()


def update_kernel(entries, chunks, split, slots, total, vgrad, *refs):
    run_update(entries, split, slots, total, vgrad, refs[:chunks], refs[chunks : 2 * chunks], *refs[2 * chunks :])


def run_update(
    entries,
    split,
    slots,
    total,
    vgrad,
    egrads,
    emoms,
    ew_ref,
    vm_ref,
    vw_ref,
    ew_out,
    em_out,
    vw_out,
    vm_out,
    weights,
    vmom,
    vweights,
    em_stage,
    ew_stage,
    vm_stage,
    vw_stage,
    in_sem,
    out_sem,
    v_sem,
):
    tile = egrads[0].shape[0] // split
    tiles = len(egrads) * split

    def weight_in(t):
        rs = pl.ds(t * tile, tile)
        return pltpu.make_async_copy(ew_ref.at[rs], weights.at[rs], in_sem.at[t])

    def out(t):
        rs = pl.ds(t * tile, tile)
        slot = t % slots
        return (
            pltpu.make_async_copy(em_stage.at[slot], em_out.at[rs], out_sem.at[slot, 0]),
            pltpu.make_async_copy(ew_stage.at[slot], ew_out.at[rs], out_sem.at[slot, 1]),
        )

    for t in range(tiles):
        weight_in(t).start()
    v_in = (
        pltpu.make_async_copy(vm_ref, vmom, v_sem.at[0]),
        pltpu.make_async_copy(vw_ref, vweights, v_sem.at[1]),
    )
    v_out = (
        pltpu.make_async_copy(vm_stage, vm_out, v_sem.at[2]),
        pltpu.make_async_copy(vw_stage, vw_out, v_sem.at[3]),
    )
    for copy in v_in:
        copy.start()
    factor = jnp.minimum(1.0, math.sqrt(entries) / jnp.sqrt(total[0:1, 0:1] + 1e-06))
    for t in range(tiles):
        rs = pl.ds(t * tile, tile)
        slot = t % slots
        if t >= slots:
            for copy in out(t - slots):
                copy.wait()
        weight_in(t).wait()
        inner = pl.ds(t % split * tile, tile)
        moment = MOMENTUM_DECAY * emoms[t // split][inner] + factor * egrads[t // split][inner]
        em_stage[slot] = moment
        ew_stage[slot] = (weights[rs].astype(F32) - STEP_RATE * moment).astype(BF16)
        for copy in out(t):
            copy.start()
    for copy in v_in:
        copy.wait()
    moment = MOMENTUM_DECAY * vmom[...] + factor * vgrad[...]
    vm_stage[...] = moment
    vw_stage[...] = (vweights[...].astype(F32) - STEP_RATE * moment).astype(BF16)
    for copy in v_out:
        copy.start()
    for t in range(max(tiles - slots, 0), tiles):
        for copy in out(t):
            copy.wait()
    for copy in v_out:
        copy.wait()


def on_device(
    normed_inputs,
    value_cotangent,
    expert_hidden,
    expert_cotangent,
    slot_gate,
    slot_count,
    expert_weight,
    expert_moment,
    value_weight,
    value_moment,
):
    n_section = lax.axis_size("section")
    n_wide = lax.axis_size("wide")
    n_narrow = lax.axis_size("narrow")
    width, kv = normed_inputs.shape[-1], value_cotangent.shape[-1]
    x = normed_inputs.reshape(-1, width)
    vc = value_cotangent.reshape(-1, kv)
    hidden = expert_hidden.reshape(-1, expert_hidden.shape[-1])
    cotangent = expert_cotangent[0, 0]
    micro, slots, _ = cotangent.shape
    positions = lax.axis_index("wide") * slots + jnp.arange(slots, dtype=jnp.int32)
    live = positions[None, :] < slot_count[0, 0][:, None]
    coefficient = jnp.where(live, slot_gate[0, 0].astype(F32), 0.0)
    coefficient = jnp.broadcast_to(coefficient[:, :, None], (micro, slots, 128))

    tokens = x.shape[0]
    h_rows, ff = hidden.shape
    chunks = column_chunks(ff)
    r_width = width // (n_wide * n_narrow)
    s_width = width // n_narrow
    piece = RS_PIECES
    peers = n_wide * n_narrow - 1 + n_section - 1
    dma = pltpu.SemaphoreType.DMA
    hbm = pl.BlockSpec(memory_space=pl.ANY)
    vmem = pl.BlockSpec(memory_space=pltpu.VMEM)
    block = pltpu.VMEM((ff // chunks, s_width), F32)
    scratch = [
        pltpu.VMEM((chunks, n_narrow * h_rows, ff // chunks), BF16),
        pltpu.VMEM((n_narrow, micro, n_wide, slots, s_width), BF16),
        pltpu.VMEM((micro, slots, width), BF16),
        pltpu.VMEM((n_narrow, n_wide * tokens, r_width), BF16),
        pltpu.VMEM((n_wide * tokens, kv), BF16),
        pltpu.VMEM((n_narrow, r_width, kv), BF16),
        pltpu.VMEM((n_narrow, r_width, kv), BF16),
        pltpu.VMEM((r_width, kv), BF16),
        pltpu.VMEM((peers, 8, 128), F32),
        pltpu.VMEM((8, 128), F32),
    ]
    *blocks, vgrad, total = pl.pallas_call(
        functools.partial(gather_kernel, (n_section, n_wide, n_narrow, chunks)),
        out_shape=(
            *[block] * (2 * chunks),
            pltpu.VMEM((r_width, kv), F32),
            pltpu.VMEM((8, 128), F32),
        ),
        in_specs=[hbm, hbm, hbm, vmem, vmem, hbm],
        out_specs=(vmem,) * (2 * chunks + 2),
        scratch_shapes=[
            *scratch,
            dma((n_narrow, chunks)),
            dma((n_narrow, chunks)),
            dma((n_narrow, chunks)),
            dma((n_narrow, n_wide)),
            dma((n_narrow,)),
            dma((n_narrow, n_wide)),
            dma((n_wide, n_narrow + 1)),
            dma((n_wide, n_narrow + 1)),
            dma((n_narrow, piece)),
            dma((piece,)),
            dma((n_narrow, piece)),
            dma((n_narrow, piece)),
            dma((peers,)),
            dma((peers,)),
            dma((1 + n_narrow + 2 * chunks,)),
        ],
        compiler_params=pltpu.CompilerParams(
            collective_id=0, has_side_effects=True, vmem_limit_bytes=grant(scratch, cotangent, coefficient)
        ),
    )(x, vc, hidden, cotangent, coefficient, expert_moment[0])

    total, vgrad, *blocks = (
        pltpu.with_memory_space_constraint(a, pltpu.VMEM) for a in (total, vgrad, *blocks)
    )
    layer_entries = ff * s_width + r_width * kv
    entries = n_section * n_wide * n_narrow * layer_entries
    split, depth = 2, 4
    tiles = chunks * split
    tile = ff // tiles
    update_scratch = [
        pltpu.VMEM((ff, s_width), BF16),
        pltpu.VMEM((r_width, kv), F32),
        pltpu.VMEM((r_width, kv), BF16),
        pltpu.VMEM((depth, tile, s_width), F32),
        pltpu.VMEM((depth, tile, s_width), BF16),
        pltpu.VMEM((r_width, kv), F32),
        pltpu.VMEM((r_width, kv), BF16),
    ]
    outs = pl.pallas_call(
        functools.partial(update_kernel, entries, chunks, split, depth),
        out_shape=(
            jax.ShapeDtypeStruct((ff, s_width), BF16),
            jax.ShapeDtypeStruct((ff, s_width), F32),
            jax.ShapeDtypeStruct((r_width, kv), BF16),
            jax.ShapeDtypeStruct((r_width, kv), F32),
        ),
        in_specs=[vmem] * (2 * chunks + 2) + [hbm] * 3,
        out_specs=(hbm, hbm, hbm, hbm),
        scratch_shapes=[
            *update_scratch,
            dma((tiles,)),
            dma((depth, 2)),
            dma((4,)),
        ],
        compiler_params=pltpu.CompilerParams(vmem_limit_bytes=grant(update_scratch)),
    )(total, vgrad, *blocks, expert_weight[0], value_moment[0], value_weight[0])
    return tuple(o[None] for o in outs)


def solution(mesh):
    return jax.shard_map(
        on_device,
        mesh=mesh,
        in_specs=(
            P("section", "narrow", None, "wide", None),
            P("section", "narrow", None, "wide", None),
            P("section", "narrow", None, None, "wide"),
            P("section", "narrow", None, "wide", None),
            P("section", "narrow", None, "wide"),
            P("section", "narrow", None),
            P("section", "wide", "narrow"),
            P("section", "wide", "narrow"),
            P("section", ("wide", "narrow"), None),
            P("section", ("wide", "narrow"), None),
        ),
        out_specs=(
            P("section", "wide", "narrow"),
            P("section", "wide", "narrow"),
            P("section", ("wide", "narrow"), None),
            P("section", ("wide", "narrow"), None),
        ),
        check_vma=False,
    )
```

profile of v0, /device:TPU:0, one launch (start us, length us, event | category | flops | bytes accessed | tf_op | source)
XLA Modules:
  0.0 187.9 jit_solution(10972053003290413183)
XLA Ops:
  0.6 0.8 convert_select_fusion
  1.4 0.7 broadcast_in_dim.24.coef_ref
  2.1 0.0 copy-start
  2.1 174.6 %shard_map.129 = (f32[512,1024]{1,0:T(8,128)S(1)}, f32[512,1024]{1,0:T(8,128)S(1)}, f32[512,1024]{1,0:T(8,128)S(1)}, f32[512,1024]{1,0:T(8,128)S(1)}, f32[512,10...) custom-call(bf16[384,4096]{1,0:T(8,128)(2,1)} %bitcast.19, ...), custom_call_target="tpu_custom_call" | custom-call | tf_op jit(solution)/shard_map/pallas_call | solution.py:563
  176.7 0.0 copy-done
  176.7 11.0 %shard_map.130 = (bf16[3584,1024]{1,0:T(8,128)(2,1)}, f32[3584,1024]{1,0:T(8,128)}, bf16[512,1024]{1,0:T(8,128)(2,1)}, f32[512,1024]{1,0:T(8,128)}) custom-call(f32[8,128]{1,0:T(8,128)S(1)} %get-tuple-element.24.total, f32[512,1024]{1,0:T(8,128)S(1)} %get-tuple-element.25.vgrad, f32[512,1024]{1,0:T(8,128)S(1)} %get-tuple-element.26.refs_0_, ...), custom_call_target="tpu_custom_call" | custom-call | tf_op jit(solution)/shard_map/pallas_call | solution.py:612
  (1 shorter events, 0.0 us)
Async XLA Ops:
  2.1 174.6 %copy-start = (bf16[1,512,1024]{2,1,0:T(8,128)(2,1)S(1)}, bf16[1,512,1024]{2,1,0:T(8,128)(2,1)}, u32[]{:S(2)}) copy-start(bf16[1,512,1024]{2,1,0:T(8,128)(2,1)} %param.18) | copy-start | bytes 3145732
where the time goes:
time: 188 us
  Pallas kernels  186 us (99%)
    pallas_call x1, Pallas kernels, on_device(): pl.pallas_call(functools.partial(gather_kernel, (n_section, n_wide, n_nar...  175 us
    pallas_call x1, Pallas kernels, on_device(): pl.pallas_call(functools.partial(update_kernel, entries, chunks, split, d...  11 us

commit v1 on v0

--- a/solution.py
+++ b/solution.py
@@ -24,7 +24,7 @@
 def grant(scratch, *arrays):
     held = [(math.prod(a.shape), a.dtype) for a in arrays]
     held += [(math.prod(a.inner_aval.shape), a.inner_aval.dtype) for a in scratch]
-    return sum(n * d.itemsize for n, d in held) + 2 * 2**20
+    return sum(n * d.itemsize for n, d in held) + 4 * 2**20
 
 
 def dot_rows(a, b):
@@ -37,13 +37,16 @@
     vc_ref,
     h_ref,
     cot_ref,
-    coef_ref,
+    gate_ref,
+    count_ref,
     mom_ref,
+    w_ref,
     *refs,
 ):
     n_section, n_wide, n_narrow, chunks = dims
+    arrays = (x_ref, vc_ref, h_ref, cot_ref, gate_ref, count_ref, mom_ref, w_ref)
     egrads, emoms, refs = refs[:chunks], refs[chunks : 2 * chunks], refs[2 * chunks :]
-    run_gather(dims, x_ref, vc_ref, h_ref, cot_ref, coef_ref, mom_ref, egrads, emoms, *refs)
+    run_gather(dims, *arrays, egrads, emoms, refs[:chunks], *refs[chunks:])
 
 
 def run_gather(
@@ -52,13 +55,15 @@
     vc_ref,
     h_ref,
     cot_ref,
-    coef_ref,
+    gate_ref,
+    count_ref,
     mom_ref,
+    w_ref,
     egrads,
     emoms,
+    hbuf,
     vgrad,
     total,
-    hbuf,
     sbuf,
     scaled,
     rows,
@@ -67,6 +72,7 @@
     rbuf,
     rlast,
     sums,
+    own_sum,
     mine,
     h_recv,
     h_right,
@@ -114,10 +120,14 @@
         )
 
     right, left = (si, wi, jnp.minimum(ni + 1, last)), (si, wi, jnp.maximum(ni - 1, 0))
-    groups = [
-        [(0, w, n) for w in range(n_wide) for n in range(n_narrow) if w or n],
-        [(s, 0, 0) for s in range(1, n_section)],
-    ]
+    n_devices = n_section * n_wide * n_narrow
+    greeted = [(s, 0, 0) for s in range(1, n_section)]
+    greeted += [(0, w, 0) for w in range(1, n_wide)]
+    greeted += [(0, 0, n) for n in range(1, n_narrow)]
+
+    barrier = pltpu.get_barrier_semaphore()
+    for offset in greeted:
+        pl.semaphore_signal(barrier, inc=1, device_id=at(*offset), device_id_type=MESH)
 
     own = []
     own.append(
@@ -135,7 +145,7 @@
     own_hidden = [
         pltpu.make_async_copy(
             h_ref.at[:, pl.ds(c * c_width, c_width)],
-            hbuf.at[c, pl.ds(ni * h_rows, h_rows)],
+            hbuf[c].at[pl.ds(ni * h_rows, h_rows)],
             local.at[1 + n_narrow + c],
         )
         for c in range(chunks)
@@ -148,19 +158,24 @@
         )
         for c in range(chunks)
     ]
-    for copy in own + own_hidden:
+    own_slots = pltpu.make_async_copy(cot_ref, scaled, local.at[1 + n_narrow + 2 * chunks])
+    blocks = s_width // c_width
+    own_weights = [
+        pltpu.make_async_copy(
+            w_ref.at[pl.ds(c * c_width, c_width), pl.ds(j * c_width, c_width)],
+            hbuf[c].at[pl.ds(j * c_width, c_width)],
+            local.at[2 + n_narrow + 2 * chunks + c * blocks + j],
+        )
+        for c in range(chunks)
+        for j in range(blocks)
+    ]
+    for copy in [own_slots] + own + own_hidden:
         copy.start()
 
-    barrier = pltpu.get_barrier_semaphore()
-    n_peers = 0
-    for group in groups:
-        for offset in group:
-            pl.semaphore_signal(barrier, inc=1, device_id=at(*offset), device_id_type=MESH)
-            n_peers += 1
-    pl.semaphore_wait(barrier, n_peers)
+    pl.semaphore_wait(barrier, len(greeted))
 
     def hidden_copy(r, c, rightward, first):
-        block = hbuf.at[c, pl.ds(r * h_rows, h_rows)]
+        block = hbuf[c].at[pl.ds(r * h_rows, h_rows)]
         src = h_ref.at[:, pl.ds(c * c_width, c_width)] if first else block
         sems = h_right if rightward else h_left
         return remote(src, block, sems.at[r, c], h_recv.at[r, c], right if rightward else left)
@@ -234,15 +249,23 @@
     def slot_arrival(r, w):
         return remote(sbuf.at[r, :, w], sbuf.at[r, :, w], s_send.at[0], s_recv.at[r, w], right)
 
+    for c in range(0, 2):
+        send_own_hidden(c)
     for k in range(1, n_wide):
         wide_vc(k, wi).start()
     for d in dest_order:
         for k in range(1, n_wide):
             wide_rows(k, d, wi).start()
-    for c in range(0, 2):
-        send_own_hidden(c)
-
-    scaled[...] = (coef_ref[:, :, 0:1] * cot_ref[...].astype(F32)).astype(BF16)
+
+    own_slots.wait()
+    slots = scaled.shape[1]
+    down = lax.broadcasted_iota(jnp.int32, (slots, slots), 0)
+    across = lax.broadcasted_iota(jnp.int32, (slots, slots), 1)
+    for m in range(scaled.shape[0]):
+        live = wi * slots + across < count_ref[0:1, m : m + 1]
+        gates = jnp.where(live & (down == across), gate_ref[m : m + 1, :].astype(F32), 0.0)
+        coefficient = jnp.sum(gates, axis=1, keepdims=True)
+        scaled[m] = (coefficient * scaled[m].astype(F32)).astype(BF16)
     for k in range(1, n_narrow):
         slot_copy(k).start()
     for c in range(2, chunks):
@@ -264,6 +287,17 @@
             wide_rows(k, d, lax.rem(wi + n_wide - k, n_wide)).wait_recv()
         part[d] = dot_rows(rows[d], cots[...]).astype(BF16)
 
+    mine[...] = jnp.zeros_like(mine)
+
+    def add_squares(block):
+        sq = block * block
+        n_rows, n_cols = sq.shape
+        folded = jnp.sum(sq.reshape(n_rows // 8, 8, n_cols), axis=0)
+        acc = folded[:, 0:128]
+        for lane in range(128, n_cols, 128):
+            acc = acc + folded[:, lane : lane + 128]
+        mine[...] += acc
+
     def piece_at(ref, d, q):
         return ref.at[d, pl.ds(q * piece, piece)]
 
@@ -296,7 +330,10 @@
                         rs = pl.ds(q * piece, piece)
                         came = rlast[rs] if landing else rbuf[d, rs]
                         if final:
-                            vgrad[rs] += came.astype(F32)
+                            done = vgrad[rs] + came.astype(F32)
+                            vgrad[rs] = done
+                            if me in (0, last) or rightward == (2 * me > last):
+                                add_squares(done)
                         else:
                             part[d, rs] = (part[d, rs].astype(F32) + came.astype(F32)).astype(BF16)
                             ahead = me + 1 if rightward else me - 1
@@ -315,21 +352,10 @@
             def _():
                 sum_send(last, d, False)
 
-    mine[...] = jnp.zeros_like(mine)
-
-    def add_squares(block):
-        sq = block * block
-        n_rows, n_cols = sq.shape
-        folded = jnp.sum(sq.reshape(n_rows // 8, 8, n_cols), axis=0)
-        acc = folded[:, 0:128]
-        for lane in range(128, n_cols, 128):
-            acc = acc + folded[:, lane : lane + 128]
-        mine[...] += acc
-
     right_side = sbuf.at[...]
 
     def expert_chunk(c):
-        product = dot_rows(hbuf[c], right_side[...].reshape(-1, s_width))
+        product = dot_rows(hbuf[c][...], right_side[...].reshape(-1, s_width))
         egrads[c][...] = product
         add_squares(product)
 
@@ -376,25 +402,20 @@
                 expert_chunk(c)
                 if c % 2 == 1:
                     sum_slot(1 + c // 2)
-    sum_slot(4)
-    add_squares(vgrad[...])
-
-    index = 0
-    for group in groups:
-        base = index
-        for offset in group:
-            remote(mine, sums.at[index], g_send.at[index], g_recv.at[index], at(*offset)).start()
-            index += 1
-        for i in range(base, index):
-            remote(mine, sums.at[i], g_send.at[i], g_recv.at[i], right).wait_send()
-        for i in range(base, index):
-            remote(mine, sums.at[i], g_send.at[i], g_recv.at[i], right).wait_recv()
-        mine[...] = mine[...] + jnp.sum(sums[base:index], axis=0)
-    overall = jnp.sum(mine[...])
-    total[...] = jnp.zeros_like(total) + overall
-
-    for copy in own_moment:
-        copy.wait()
+    sum_slot(2 * (last - 1))
+
+    def sum_out(p):
+        peer = lax.rem((si * n_wide + wi) * n_narrow + ni + p, n_devices)
+        device = (
+            lax.div(peer, n_wide * n_narrow),
+            lax.rem(lax.div(peer, n_narrow), n_wide),
+            lax.rem(peer, n_narrow),
+        )
+        return remote(own_sum, sums.at[p], g_send.at[p], g_recv.at[p], device)
+
+    own_sum[...] = jnp.sum(mine[...], axis=0, keepdims=True)
+    sums[0] = own_sum[...]
+    lax.fori_loop(1, n_devices, lambda p, _: [sum_out(p).start()] and 0, 0)
     for c in range(chunks):
         for k in range(n_narrow):
 
@@ -405,6 +426,8 @@
             @pl.when((ni + k <= last) & (ni > 0))
             def _(k=k, c=c):
                 hidden_copy(ni + k, c, False, False).wait_send()
+    for copy in own_weights:
+        copy.start()
 
     for k in range(1, n_wide):
         wide_vc(k, wi).wait_send()
@@ -424,10 +447,18 @@
             @pl.when(ni > d)
             def _(d=d, q=q):
                 sum_copy(d, q, False, False).wait_send()
+    for copy in own_moment:
+        copy.wait()
+    lax.fori_loop(1, n_devices, lambda p, _: [sum_out(p).wait_send()] and 0, 0)
+    lax.fori_loop(1, n_devices, lambda p, _: [sum_out(p).wait_recv()] and 0, 0)
+    total[...] = jnp.zeros_like(total) + jnp.sum(sums[...])
+    for copy in own_weights:
+        copy.wait()
 
 
 def update_kernel(entries, chunks, split, slots, total, vgrad, *refs):
-    run_update(entries, split, slots, total, vgrad, refs[:chunks], refs[chunks : 2 * chunks], *refs[2 * chunks :])
+    egrads, emoms, refs = refs[:chunks], refs[chunks : 2 * chunks], refs[2 * chunks :]
+    run_update(entries, split, slots, total, vgrad, egrads, emoms, refs[:chunks], *refs[chunks:])
 
 
 def run_update(
@@ -438,30 +469,26 @@
     vgrad,
     egrads,
     emoms,
-    ew_ref,
+    weights,
     vm_ref,
     vw_ref,
     ew_out,
     em_out,
     vw_out,
     vm_out,
-    weights,
     vmom,
     vweights,
     em_stage,
     ew_stage,
     vm_stage,
     vw_stage,
-    in_sem,
     out_sem,
     v_sem,
 ):
     tile = egrads[0].shape[0] // split
     tiles = len(egrads) * split
 
-    def weight_in(t):
-        rs = pl.ds(t * tile, tile)
-        return pltpu.make_async_copy(ew_ref.at[rs], weights.at[rs], in_sem.at[t])
+    c_width = weights[0].shape[1]
 
     def out(t):
         rs = pl.ds(t * tile, tile)
@@ -471,8 +498,6 @@
             pltpu.make_async_copy(ew_stage.at[slot], ew_out.at[rs], out_sem.at[slot, 1]),
         )
 
-    for t in range(tiles):
-        weight_in(t).start()
     v_in = (
         pltpu.make_async_copy(vm_ref, vmom, v_sem.at[0]),
         pltpu.make_async_copy(vw_ref, vweights, v_sem.at[1]),
@@ -485,16 +510,18 @@
         copy.start()
     factor = jnp.minimum(1.0, math.sqrt(entries) / jnp.sqrt(total[0:1, 0:1] + 1e-06))
     for t in range(tiles):
-        rs = pl.ds(t * tile, tile)
         slot = t % slots
         if t >= slots:
             for copy in out(t - slots):
                 copy.wait()
-        weight_in(t).wait()
-        inner = pl.ds(t % split * tile, tile)
-        moment = MOMENTUM_DECAY * emoms[t // split][inner] + factor * egrads[t // split][inner]
-        em_stage[slot] = moment
-        ew_stage[slot] = (weights[rs].astype(F32) - STEP_RATE * moment).astype(BF16)
+        c, row = t // split, t % split * tile
+        inner = pl.ds(row, tile)
+        for j in range(em_stage.shape[2] // c_width):
+            cols = pl.ds(j * c_width, c_width)
+            moment = MOMENTUM_DECAY * emoms[c][inner, cols] + factor * egrads[c][inner, cols]
+            weight = weights[c][pl.ds(j * c_width + row, tile)]
+            em_stage[slot, :, cols] = moment
+            ew_stage[slot, :, cols] = (weight.astype(F32) - STEP_RATE * moment).astype(BF16)
         for copy in out(t):
             copy.start()
     for copy in v_in:
@@ -532,24 +559,20 @@
     hidden = expert_hidden.reshape(-1, expert_hidden.shape[-1])
     cotangent = expert_cotangent[0, 0]
     micro, slots, _ = cotangent.shape
-    positions = lax.axis_index("wide") * slots + jnp.arange(slots, dtype=jnp.int32)
-    live = positions[None, :] < slot_count[0, 0][:, None]
-    coefficient = jnp.where(live, slot_gate[0, 0].astype(F32), 0.0)
-    coefficient = jnp.broadcast_to(coefficient[:, :, None], (micro, slots, 128))
-
+    in_hbm = functools.partial(pltpu.with_memory_space_constraint, memory_space=pltpu.HBM)
     tokens = x.shape[0]
     h_rows, ff = hidden.shape
     chunks = column_chunks(ff)
     r_width = width // (n_wide * n_narrow)
     s_width = width // n_narrow
     piece = RS_PIECES
-    peers = n_wide * n_narrow - 1 + n_section - 1
+    n_devices = n_section * n_wide * n_narrow
     dma = pltpu.SemaphoreType.DMA
-    hbm = pl.BlockSpec(memory_space=pl.ANY)
+    hbm = pl.BlockSpec(memory_space=pltpu.HBM)
     vmem = pl.BlockSpec(memory_space=pltpu.VMEM)
     block = pltpu.VMEM((ff // chunks, s_width), F32)
+    w_block = pltpu.VMEM((n_narrow * h_rows, ff // chunks), BF16)
     scratch = [
-        pltpu.VMEM((chunks, n_narrow * h_rows, ff // chunks), BF16),
         pltpu.VMEM((n_narrow, micro, n_wide, slots, s_width), BF16),
         pltpu.VMEM((micro, slots, width), BF16),
         pltpu.VMEM((n_narrow, n_wide * tokens, r_width), BF16),
@@ -557,18 +580,20 @@
         pltpu.VMEM((n_narrow, r_width, kv), BF16),
         pltpu.VMEM((n_narrow, r_width, kv), BF16),
         pltpu.VMEM((r_width, kv), BF16),
-        pltpu.VMEM((peers, 8, 128), F32),
+        pltpu.VMEM((n_devices, 1, 128), F32),
+        pltpu.VMEM((1, 128), F32),
         pltpu.VMEM((8, 128), F32),
     ]
     *blocks, vgrad, total = pl.pallas_call(
         functools.partial(gather_kernel, (n_section, n_wide, n_narrow, chunks)),
         out_shape=(
             *[block] * (2 * chunks),
+            *[w_block] * chunks,
             pltpu.VMEM((r_width, kv), F32),
             pltpu.VMEM((8, 128), F32),
         ),
-        in_specs=[hbm, hbm, hbm, vmem, vmem, hbm],
-        out_specs=(vmem,) * (2 * chunks + 2),
+        in_specs=[hbm, hbm, hbm, hbm, vmem, vmem, hbm, hbm],
+        out_specs=(vmem,) * (3 * chunks + 2),
         scratch_shapes=[
             *scratch,
             dma((n_narrow, chunks)),
@@ -583,14 +608,20 @@
             dma((piece,)),
             dma((n_narrow, piece)),
             dma((n_narrow, piece)),
-            dma((peers,)),
-            dma((peers,)),
-            dma((1 + n_narrow + 2 * chunks,)),
+            dma((n_devices,)),
+            dma((n_devices,)),
+            dma((2 + n_narrow + (2 + s_width * chunks // ff) * chunks,)),
         ],
         compiler_params=pltpu.CompilerParams(
-            collective_id=0, has_side_effects=True, vmem_limit_bytes=grant(scratch, cotangent, coefficient)
+            collective_id=0, has_side_effects=True, vmem_limit_bytes=grant(scratch)
         ),
-    )(x, vc, hidden, cotangent, coefficient, expert_moment[0])
+    )(
+        *(in_hbm(a) for a in (x, vc, hidden, cotangent)),
+        slot_gate[0, 0],
+        slot_count[0],
+        in_hbm(expert_moment[0]),
+        in_hbm(expert_weight[0]),
+    )
 
     total, vgrad, *blocks = (
         pltpu.with_memory_space_constraint(a, pltpu.VMEM) for a in (total, vgrad, *blocks)
@@ -601,7 +632,6 @@
     tiles = chunks * split
     tile = ff // tiles
     update_scratch = [
-        pltpu.VMEM((ff, s_width), BF16),
         pltpu.VMEM((r_width, kv), F32),
         pltpu.VMEM((r_width, kv), BF16),
         pltpu.VMEM((depth, tile, s_width), F32),
@@ -617,16 +647,15 @@
             jax.ShapeDtypeStruct((r_width, kv), BF16),
             jax.ShapeDtypeStruct((r_width, kv), F32),
         ),
-        in_specs=[vmem] * (2 * chunks + 2) + [hbm] * 3,
+        in_specs=[vmem] * (3 * chunks + 2) + [hbm] * 2,
         out_specs=(hbm, hbm, hbm, hbm),
         scratch_shapes=[
             *update_scratch,
-            dma((tiles,)),
             dma((depth, 2)),
             dma((4,)),
         ],
         compiler_params=pltpu.CompilerParams(vmem_limit_bytes=grant(update_scratch)),
-    )(total, vgrad, *blocks, expert_weight[0], value_moment[0], value_weight[0])
+    )(total, vgrad, *blocks, *(in_hbm(a[0]) for a in (value_moment, value_weight)))
     return tuple(o[None] for o in outs)
 
 

time: 188 us -> 182 us (0.968)
  Pallas kernels: 186 us -> 181 us
    pallas_call x1, Pallas kernels: 175 us -> 172 us  [on_device(): pl.pallas_call(functools.partial(gather_kernel, (n_section, n_wide, n_nar...]
    pallas_call x1, Pallas kernels: 11 us -> 8.96 us  [on_device(): pl.pallas_call(functools.partial(update_kernel, entries, chunks, split, d...]
where the time goes in v1:
time: 182 us
  Pallas kernels  181 us (99%)
    pallas_call x1, Pallas kernels, on_device(): pl.pallas_call(functools.partial(gather_kernel, (n_section, n_wide, n_nar...  172 us
    pallas_call x1, Pallas kernels, on_device(): pl.pallas_call(functools.partial(update_kernel, entries, chunks, split, d...  8.96 us

profile of v1, /device:TPU:0, one launch (start us, length us, event | category | flops | bytes accessed | tf_op | source)
XLA Modules:
  0.0 181.9 jit_solution(18112402185945219372)
XLA Ops:
  0.6 172.2 %shard_map.129 = (f32[512,1024]{1,0:T(8,128)S(1)}, f32[512,1024]{1,0:T(8,128)S(1)}, f32[512,1024]{1,0:T(8,128)S(1)}, f32[512,1024]{1,0:T(8,128)S(1)}, f32[512,10...) custom-call(bf16[384,4096]{1,0:T(8,128)(2,1)} %bitcast.16, ...), custom_call_target="tpu_custom_call" | custom-call | tf_op jit(solution)/shard_map/pallas_call | solution.py:587
  172.8 9.0 %shard_map.130 = (bf16[3584,1024]{1,0:T(8,128)(2,1)}, f32[3584,1024]{1,0:T(8,128)}, bf16[512,1024]{1,0:T(8,128)(2,1)}, f32[512,1024]{1,0:T(8,128)}) custom-call(f32[8,128]{1,0:T(8,128)S(1)} %get-tuple-element.31.total, f32[512,1024]{1,0:T(8,128)S(1)} %get-tuple-element.32.vgrad, f32[512,1024]{1,0:T(8,128)S(1)} %get-tuple-element.33.refs_0_, ...), custom_call_target="tpu_custom_call" | custom-call | tf_op jit(solution)/shard_map/pallas_call | solution.py:642

commit v2 on v1

--- a/solution.py
+++ b/solution.py
@@ -13,7 +13,7 @@
 MESH = pl.DeviceIdType.MESH
 F32 = jnp.float32
 BF16 = jnp.bfloat16
-RS_PIECES = 2
+RS_PIECES = 4
 
 
 def column_chunks(width):
@@ -89,6 +89,9 @@
     g_recv,
     g_send,
     local,
+    p_recv,
+    p_send,
+    spare,
 ):
     n_section, n_wide, n_narrow, chunks = dims
     si, wi, ni = lax.axis_index("section"), lax.axis_index("wide"), lax.axis_index("narrow")
@@ -178,7 +181,7 @@
         block = hbuf[c].at[pl.ds(r * h_rows, h_rows)]
         src = h_ref.at[:, pl.ds(c * c_width, c_width)] if first else block
         sems = h_right if rightward else h_left
-        return remote(src, block, sems.at[r, c], h_recv.at[r, c], right if rightward else left)
+        return remote(src, block, sems.at[c], h_recv.at[r, c], right if rightward else left)
 
     def send_own_hidden(c):
         @pl.when(ni < last)
@@ -305,7 +308,7 @@
         dst = rlast.at[pl.ds(q * piece, piece)] if final else piece_at(rbuf, d, q)
         sem = r_last.at[q] if final else r_recv.at[d, q]
         sems = r_right if rightward else r_left
-        return remote(piece_at(part, d, q), dst, sems.at[d, q], sem, right if rightward else left)
+        return remote(piece_at(part, d, q), dst, sems.at[d], sem, right if rightward else left)
 
     def sum_send(i, d, rightward):
         final_right = rightward and d == i + 1
@@ -332,12 +335,49 @@
                         if final:
                             done = vgrad[rs] + came.astype(F32)
                             vgrad[rs] = done
-                            if me in (0, last) or rightward == (2 * me > last):
+                            if me not in (0, last) and rightward == (2 * me > last):
                                 add_squares(done)
                         else:
                             part[d, rs] = (part[d, rs].astype(F32) + came.astype(F32)).astype(BF16)
                             ahead = me + 1 if rightward else me - 1
-                            sum_copy(d, q, rightward, rightward and d == ahead).start()
+                            if ahead not in (0, last) or q < RS_PIECES - 1:
+                                sum_copy(d, q, rightward, rightward and d == ahead).start()
+
+    def edge_part(rightward):
+        return remote(
+            part.at[0 if rightward else last],
+            cots.at[pl.ds(0, r_width)],
+            p_send.at[0],
+            p_recv.at[0],
+            right if rightward else left,
+        )
+
+    def grant_spare():
+        @pl.when(ni == 1)
+        def _():
+            pl.semaphore_signal(spare, inc=1, device_id=left, device_id_type=MESH)
+
+        @pl.when(ni == last - 1)
+        def _():
+            pl.semaphore_signal(spare, inc=1, device_id=right, device_id_type=MESH)
+
+    def send_edge_part():
+        for edge in (0, last):
+
+            @pl.when(ni == edge)
+            def _(edge=edge):
+                pl.semaphore_wait(spare, 1)
+                edge_part(edge == 0).start()
+
+    def edge_squares():
+        for me, d in ((1, 0), (last - 1, last)):
+
+            @pl.when(ni == me)
+            def _(d=d):
+                edge_part(d == 0).wait_recv()
+                for q in range(RS_PIECES):
+                    rs = pl.ds(q * piece, piece)
+                    add_squares(part[d, rs].astype(F32) + cots[rs].astype(F32))
 
     def originate(d):
         if d > 0:
@@ -384,8 +424,10 @@
                         def _(d=d):
                             sum_send(last, d, False)
 
+                grant_spare()
                 vgrad[...] = part[ni].astype(F32)
             if k == 2 and c == 3:
+                send_edge_part()
                 for j in range(1, n_narrow):
                     r = lax.rem(ni + n_narrow - j, n_narrow)
                     slot_arrival(r, wi).wait_recv()
@@ -402,7 +444,7 @@
                 expert_chunk(c)
                 if c % 2 == 1:
                     sum_slot(1 + c // 2)
-    sum_slot(2 * (last - 1))
+    edge_squares()
 
     def sum_out(p):
         peer = lax.rem((si * n_wide + wi) * n_narrow + ni + p, n_devices)
@@ -411,23 +453,42 @@
             lax.rem(lax.div(peer, n_narrow), n_wide),
             lax.rem(peer, n_narrow),
         )
-        return remote(own_sum, sums.at[p], g_send.at[p], g_recv.at[p], device)
+        return remote(own_sum, sums.at[p], g_send.at[0], g_recv.at[0], device)
+
+    def all_sums():
+        others = sums.at[pl.ds(1, n_devices - 1)]
+        return remote(others, others, g_send.at[0], g_recv.at[0], right)
 
     own_sum[...] = jnp.sum(mine[...], axis=0, keepdims=True)
     sums[0] = own_sum[...]
     lax.fori_loop(1, n_devices, lambda p, _: [sum_out(p).start()] and 0, 0)
-    for c in range(chunks):
-        for k in range(n_narrow):
-
-            @pl.when((ni >= k) & (ni < last))
-            def _(k=k, c=c):
-                hidden_copy(ni - k, c, True, False).wait_send()
-
-            @pl.when((ni + k <= last) & (ni > 0))
-            def _(k=k, c=c):
-                hidden_copy(ni + k, c, False, False).wait_send()
+    for me, d in ((1, 0), (last - 1, last)):
+
+        @pl.when(ni == me)
+        def _(d=d):
+            sum_copy(d, RS_PIECES - 1, d == last, d == last).start()
+
+    for i in range(n_narrow):
+
+        @pl.when(ni == i)
+        def _(i=i):
+            for c in range(chunks):
+                for rightward in (True, False):
+                    n_sent = i + 1 if rightward else n_narrow - i
+                    if i == (last if rightward else 0):
+                        continue
+                    sent = hbuf[c].at[pl.ds(0, n_sent * h_rows)]
+                    sem = (h_right if rightward else h_left).at[c]
+                    remote(sent, sent, sem, h_recv.at[0, c], right).wait_send()
+
     for copy in own_weights:
         copy.start()
+
+    for edge in (0, last):
+
+        @pl.when(ni == edge)
+        def _(edge=edge):
+            edge_part(edge == 0).wait_send()
 
     for k in range(1, n_wide):
         wide_vc(k, wi).wait_send()
@@ -438,22 +499,23 @@
     for k in range(1, n_narrow):
         slot_copy(k).wait_send()
     for d in range(n_narrow):
-        for q in range(RS_PIECES):
-
-            @pl.when(ni < d)
-            def _(d=d, q=q):
-                sum_copy(d, q, True, False).wait_send()
-
-            @pl.when(ni > d)
-            def _(d=d, q=q):
-                sum_copy(d, q, False, False).wait_send()
+
+        @pl.when(ni < d)
+        def _(d=d):
+            remote(part.at[d], rbuf.at[d], r_right.at[d], r_last.at[0], right).wait_send()
+
+        @pl.when(ni > d)
+        def _(d=d):
+            remote(part.at[d], rbuf.at[d], r_left.at[d], r_last.at[0], left).wait_send()
+
     for copy in own_moment:
         copy.wait()
-    lax.fori_loop(1, n_devices, lambda p, _: [sum_out(p).wait_send()] and 0, 0)
-    lax.fori_loop(1, n_devices, lambda p, _: [sum_out(p).wait_recv()] and 0, 0)
-    total[...] = jnp.zeros_like(total) + jnp.sum(sums[...])
     for copy in own_weights:
         copy.wait()
+    all_sums().wait_send()
+    sum_slot(2 * (last - 1))
+    all_sums().wait_recv()
+    total[...] = jnp.zeros_like(total) + jnp.sum(sums[...])
 
 
 def update_kernel(entries, chunks, split, slots, total, vgrad, *refs):
@@ -597,8 +659,8 @@
         scratch_shapes=[
             *scratch,
             dma((n_narrow, chunks)),
-            dma((n_narrow, chunks)),
-            dma((n_narrow, chunks)),
+            dma((chunks,)),
+            dma((chunks,)),
             dma((n_narrow, n_wide)),
             dma((n_narrow,)),
             dma((n_narrow, n_wide)),
@@ -606,11 +668,14 @@
             dma((n_wide, n_narrow + 1)),
             dma((n_narrow, piece)),
             dma((piece,)),
-            dma((n_narrow, piece)),
-            dma((n_narrow, piece)),
-            dma((n_devices,)),
-            dma((n_devices,)),
+            dma((n_narrow,)),
+            dma((n_narrow,)),
+            dma((1,)),
+            dma((1,)),
             dma((2 + n_narrow + (2 + s_width * chunks // ff) * chunks,)),
+            dma((1,)),
+            dma((1,)),
+            pltpu.SemaphoreType.REGULAR,
         ],
         compiler_params=pltpu.CompilerParams(
             collective_id=0, has_side_effects=True, vmem_limit_bytes=grant(scratch)

time: 182 us -> 176 us (0.967)
  Pallas kernels: 181 us -> 175 us
    pallas_call x1, Pallas kernels: 172 us -> 166 us  [on_device(): pl.pallas_call(functools.partial(gather_kernel, (n_section, n_wide, n_nar...]
where the time goes in v2:
time: 176 us
  Pallas kernels  175 us (99%)
    pallas_call x1, Pallas kernels, on_device(): pl.pallas_call(functools.partial(gather_kernel, (n_section, n_wide, n_nar...  166 us
    pallas_call x1, Pallas kernels, on_device(): pl.pallas_call(functools.partial(update_kernel, entries, chunks, split, d...  8.96 us

profile of v2, /device:TPU:0, one launch (start us, length us, event | category | flops | bytes accessed | tf_op | source)
XLA Modules:
  0.0 175.9 jit_solution(7460246820155834668)
XLA Ops:
  0.6 166.1 %shard_map.129 = (f32[512,1024]{1,0:T(8,128)S(1)}, f32[512,1024]{1,0:T(8,128)S(1)}, f32[512,1024]{1,0:T(8,128)S(1)}, f32[512,1024]{1,0:T(8,128)S(1)}, f32[512,10...) custom-call(bf16[384,4096]{1,0:T(8,128)(2,1)} %bitcast.16, ...), custom_call_target="tpu_custom_call" | custom-call | tf_op jit(solution)/shard_map/pallas_call | solution.py:649
  166.8 9.0 %shard_map.130 = (bf16[3584,1024]{1,0:T(8,128)(2,1)}, f32[3584,1024]{1,0:T(8,128)}, bf16[512,1024]{1,0:T(8,128)(2,1)}, f32[512,1024]{1,0:T(8,128)}) custom-call(f32[8,128]{1,0:T(8,128)S(1)} %get-tuple-element.31.total, f32[512,1024]{1,0:T(8,128)S(1)} %get-tuple-element.32.vgrad, f32[512,1024]{1,0:T(8,128)S(1)} %get-tuple-element.33.refs_0_, ...), custom_call_target="tpu_custom_call" | custom-call | tf_op jit(solution)/shard_map/pallas_call | solution.py:707

commit v3 on v2

--- a/solution.py
+++ b/solution.py
@@ -693,7 +693,7 @@
     )
     layer_entries = ff * s_width + r_width * kv
     entries = n_section * n_wide * n_narrow * layer_entries
-    split, depth = 2, 4
+    split, depth = 2, 6
     tiles = chunks * split
     tile = ff // tiles
     update_scratch = [

time: 176 us -> 176 us (level)
  no operation moved by 1% of the time
where the time goes in v3:
time: 176 us
  Pallas kernels  175 us (99%)
    pallas_call x1, Pallas kernels, on_device(): pl.pallas_call(functools.partial(gather_kernel, (n_section, n_wide, n_nar...  166 us
    pallas_call x1, Pallas kernels, on_device(): pl.pallas_call(functools.partial(update_kernel, entries, chunks, split, d...  9.34 us

profile of v3, /device:TPU:0, one launch (start us, length us, event | category | flops | bytes accessed | tf_op | source)
XLA Modules:
  0.0 176.3 jit_solution(14477757898583503052)
XLA Ops:
  0.6 166.1 %shard_map.129 = (f32[512,1024]{1,0:T(8,128)S(1)}, f32[512,1024]{1,0:T(8,128)S(1)}, f32[512,1024]{1,0:T(8,128)S(1)}, f32[512,1024]{1,0:T(8,128)S(1)}, f32[512,10...) custom-call(bf16[384,4096]{1,0:T(8,128)(2,1)} %bitcast.16, ...), custom_call_target="tpu_custom_call" | custom-call | tf_op jit(solution)/shard_map/pallas_call | solution.py:649
  166.8 9.3 %shard_map.130 = (bf16[3584,1024]{1,0:T(8,128)(2,1)}, f32[3584,1024]{1,0:T(8,128)}, bf16[512,1024]{1,0:T(8,128)(2,1)}, f32[512,1024]{1,0:T(8,128)}) custom-call(f32[8,128]{1,0:T(8,128)S(1)} %get-tuple-element.31.total, f32[512,1024]{1,0:T(8,128)S(1)} %get-tuple-element.32.vgrad, f32[512,1024]{1,0:T(8,128)S(1)} %get-tuple-element.33.refs_0_, ...), custom_call_target="tpu_custom_call" | custom-call | tf_op jit(solution)/shard_map/pallas_call | solution.py:707
